TPU v7x, 256 devices: a whole 4x4x8 slice. The times are simulated.
256 devices in a mesh: tower: 16 (over z, x_hi), dev: 16 (over x_lo, y, core).
Axes of the slice: x: 4 (x_hi: 2, x_lo: 2; x = x_hi * 2 + x_lo), y: 4, z: 8, core: 2. Of those that a mesh axis runs over, the one named last changes fastest.
Arguments:
- ids: int32 [16, 16, 2048, 32], P('tower', 'dev'), may hold values from 0 to 511
- tables: bfloat16 [16, 16, 512, 128], P('tower', 'dev'), may hold values from -1 to 1
- order: int32 [2048], replicated, may hold values from 0 to 2047, each once
- w_first: bfloat16 [16, 2048, 1024], P('tower', 'dev'), may hold values from -0.125 to 0.125
- w_second: bfloat16 [16, 1024, 512], P('tower'), may hold values from -0.1875 to 0.1875
- w_head: bfloat16 [8192, 128], replicated, may hold values from -0.0625 to 0.0625
- w_interact: float32 [256, 128], replicated, may hold values from -0.1875 to 0.1875
Outputs:
- scores: float32 [16, 128, 128], P('dev', 'tower')
Inputs may be any that keep to these rules, and one draw needn't show every extreme that they name: order is a permutation of the batch rows 0 to 2047.
All inputs are finite; a program needn't handle non-finite values.
Results may differ from a plain program's by a relative error of at most 0.0023.
Values may be sent and summed in bfloat16 or wider, within the bound.
A program may use at most 64 MiB of HBM per device.

v0:
```python
import math
import jax
import jax.numpy as jnp
from jax import lax
from jax.sharding import PartitionSpec as P


def pool_feature(feature_ids, table):
    samples = feature_ids.shape[0]
    active = table.shape[0]
    block = math.gcd(samples, 512)
    blocked = feature_ids.reshape(samples // block, block, feature_ids.shape[1])
    positions = lax.broadcasted_iota(jnp.int32, (1, 1, active), 2)

    def pool_block(block_ids):
        tally = jnp.sum((block_ids[:, :, None] == positions).astype(jnp.int32), axis=1)
        return jnp.dot(
            tally.astype(jnp.bfloat16), table, preferred_element_type=jnp.float32
        ).astype(jnp.bfloat16)

    pooled = lax.map(pool_block, blocked)
    return pooled.reshape(samples, table.shape[1])


def on_device(ids, tables, order, w_first, w_second, w_head, w_interact):
    towers = lax.axis_size("tower")
    devices = lax.axis_size("dev")
    samples = ids.shape[2]
    my_rows = samples // devices
    pieces = pool_feature(ids[0, 0], tables[0, 0])
    features = jnp.take(pieces, order, axis=0)
    received = lax.all_to_all(features, "dev", split_axis=0, concat_axis=1, tiled=True)
    preact = jnp.dot(
        received,
        lax.all_gather(w_first[0], "dev", axis=0, tiled=True),
        preferred_element_type=jnp.float32,
    )
    hidden = jnp.maximum(preact, 0.0).astype(jnp.bfloat16)
    outputs = jnp.dot(hidden, w_second[0], preferred_element_type=jnp.float32).astype(jnp.bfloat16)
    width = outputs.shape[1]
    share = my_rows // towers
    gathered = lax.all_to_all(
        outputs.reshape(1, towers, share, width), "tower", split_axis=1, concat_axis=0, tiled=True
    )[:, 0]
    amount = gathered.shape[1]
    joined = jnp.transpose(gathered, (1, 0, 2)).reshape(amount, towers * width)
    head = jnp.dot(joined, w_head, preferred_element_type=jnp.float32)
    widened = gathered.astype(jnp.float32)
    products = jnp.einsum(
        "tmz,smz->mts", widened, widened, precision=lax.Precision.HIGHEST
    ) / math.sqrt(width)
    interact_term = jnp.dot(
        products.reshape(amount, towers * towers), w_interact, precision=lax.Precision.HIGHEST
    )
    scored = head + interact_term
    return scored[None]


def solution(mesh):
    return jax.shard_map(
        on_device,
        mesh=mesh,
        in_specs=(
            P("tower", "dev", None, None),
            P("tower", "dev", None, None),
            P(),
            P("tower", "dev", None),
            P("tower", None, None),
            P(),
            P(),
        ),
        out_specs=P("dev", "tower", None),
        check_vma=False,
    )
```

profile of v0, /device:TPU:1, one launch (start us, length us, event | category | flops | bytes accessed | tf_op | source)
XLA Modules:
  0.0 118.9 jit_solution(7275496688290093356)
XLA Ops:
  6.5 0.0 copy-start
  6.5 0.0 all-gather.3.cloned.1.call-start
  6.5 0.7 all-gather.3.cloned.1.call-update
  7.3 2.3 %copy.17 = s32[1,1,2048,32]{3,2,1,0:T(8,128)} copy(s32[1,1,2048,32]{2,3,1,0:T(8,128)} %param.9) | data formatting | bytes 524288 | tf_op args[0]
  9.5 0.7 fusion.27
  10.2 53.5 %while.11 = (s32[]{:T(128)}, bf16[4,512,128]{2,1,0:T(8,128)(2,1)S(1)}, s32[4,512,32]{2,1,0:T(8,128)}, bf16[512,128]{1,0:T(8,128)(2,1)}, s32[]{:T(128)}) while((s32[]{:T(128)}, bf16[4,512,128]{2,1,0:T(8,128)(2,1)S(1)}, s32[4,512,32]{2,1,0:T(8,128)}, bf16[512,128]{1,0:T(8,128)(2,1)}, s32[]{:T(128)}) %tuple.27), condition=%wide.region_2.3_spmd.clone, body=%wide.region_0.2_spmd.clone.sunk | while | flops 92340224 | bytes 2555973 | solution.py:21
  10.2 1.0 dynamic-slice_bitcast_fusion.2
  11.2 11.1 %convert_reduce_fusion.2 = s32[512,512]{1,0:T(8,128)S(1)} fusion(s32[512,32]{1,0:T(8,128)S(1)} %dynamic-slice_bitcast_fusion.2), kind=kLoop, calls=%fused_computation.3.clone.1 | loop fusion | flops 24903680 | bytes 1114112 | tf_op jit(solution)/shard_map/while/body/eval_jaxpr/reduce_sum | solution.py:16
  22.4 1.3 %fusion.41 = bf16[4,512,128]{2,1,0:T(8,128)(2,1)S(1)} fusion(bf16[4,512,128]{2,1,0:T(8,128)(2,1)S(1)} %get-tuple-element.82, s32[]{:T(128)} %get-tuple-element.81, bf16[512,128]{1,0:T(8,128)(2,1)} %get-tuple-element.89, s32[512,512]{1,0:T(8,128)S(1)} %convert_reduce_fusion.2), kind=kOutput, calls=%fused_computation.6.clone.1 | convolution fusion | flops 67436544 | bytes 1310724 | tf_op jit(solution)/shard_map/while/body/eval_jaxpr/dot_general | solution.py:17
  23.6 1.0 dynamic-slice_bitcast_fusion.2
  24.6 11.1 %convert_reduce_fusion.2 = s32[512,512]{1,0:T(8,128)S(1)} fusion(s32[512,32]{1,0:T(8,128)S(1)} %dynamic-slice_bitcast_fusion.2), kind=kLoop, calls=%fused_computation.3.clone.1 | loop fusion | flops 24903680 | bytes 1114112 | tf_op jit(solution)/shard_map/while/body/eval_jaxpr/reduce_sum | solution.py:16
  35.7 1.3 %fusion.41 = bf16[4,512,128]{2,1,0:T(8,128)(2,1)S(1)} fusion(bf16[4,512,128]{2,1,0:T(8,128)(2,1)S(1)} %get-tuple-element.82, s32[]{:T(128)} %get-tuple-element.81, bf16[512,128]{1,0:T(8,128)(2,1)} %get-tuple-element.89, s32[512,512]{1,0:T(8,128)S(1)} %convert_reduce_fusion.2), kind=kOutput, calls=%fused_computation.6.clone.1 | convolution fusion | flops 67436544 | bytes 1310724 | tf_op jit(solution)/shard_map/while/body/eval_jaxpr/dot_general | solution.py:17
  37.0 1.0 dynamic-slice_bitcast_fusion.2
  38.0 11.1 %convert_reduce_fusion.2 = s32[512,512]{1,0:T(8,128)S(1)} fusion(s32[512,32]{1,0:T(8,128)S(1)} %dynamic-slice_bitcast_fusion.2), kind=kLoop, calls=%fused_computation.3.clone.1 | loop fusion | flops 24903680 | bytes 1114112 | tf_op jit(solution)/shard_map/while/body/eval_jaxpr/reduce_sum | solution.py:16
  49.1 1.3 %fusion.41 = bf16[4,512,128]{2,1,0:T(8,128)(2,1)S(1)} fusion(bf16[4,512,128]{2,1,0:T(8,128)(2,1)S(1)} %get-tuple-element.82, s32[]{:T(128)} %get-tuple-element.81, bf16[512,128]{1,0:T(8,128)(2,1)} %get-tuple-element.89, s32[512,512]{1,0:T(8,128)S(1)} %convert_reduce_fusion.2), kind=kOutput, calls=%fused_computation.6.clone.1 | convolution fusion | flops 67436544 | bytes 1310724 | tf_op jit(solution)/shard_map/while/body/eval_jaxpr/dot_general | solution.py:17
  50.4 1.0 dynamic-slice_bitcast_fusion.2
  51.4 11.1 %convert_reduce_fusion.2 = s32[512,512]{1,0:T(8,128)S(1)} fusion(s32[512,32]{1,0:T(8,128)S(1)} %dynamic-slice_bitcast_fusion.2), kind=kLoop, calls=%fused_computation.3.clone.1 | loop fusion | flops 24903680 | bytes 1114112 | tf_op jit(solution)/shard_map/while/body/eval_jaxpr/reduce_sum | solution.py:16
  62.5 1.3 %fusion.41 = bf16[4,512,128]{2,1,0:T(8,128)(2,1)S(1)} fusion(bf16[4,512,128]{2,1,0:T(8,128)(2,1)S(1)} %get-tuple-element.82, s32[]{:T(128)} %get-tuple-element.81, bf16[512,128]{1,0:T(8,128)(2,1)} %get-tuple-element.89, s32[512,512]{1,0:T(8,128)S(1)} %convert_reduce_fusion.2), kind=kOutput, calls=%fused_computation.6.clone.1 | convolution fusion | flops 67436544 | bytes 1310724 | tf_op jit(solution)/shard_map/while/body/eval_jaxpr/dot_general | solution.py:17
  63.8 0.0 copy-start.2
  63.8 6.2 %gather_fusion = bf16[2048,128]{1,0:T(8,128)(2,1)S(1)} fusion(bf16[2048,128]{1,0:T(8,128)(2,1)S(1)} %bitcast.58, s32[2048]{0:T(1024)S(1)} %fusion.27), kind=kCustom, calls=%fused_computation | custom fusion | bytes 1056768 | tf_op jit(solution)/shard_map/jit(_take)/gather | solution.py:31
  70.0 0.3 copy.18
  70.3 0.0 copy-done.2
  70.3 0.1 broadcast_select_fusion
  70.4 16.4 %all_to_all.25 = bf16[16,128,128]{1,2,0:T(8,128)(2,1)S(1)} all-to-all(bf16[16,128,128]{1,2,0:T(8,128)(2,1)S(1)} %broadcast_select_fusion), channel_id=1, replica_groups=mesh['tower'=16,'dev'=16] {'dev'}, dimensions={0} | all-to-all | bytes 1048576 | tf_op jit(solution)/shard_map/all_to_all | solution.py:32
  86.8 0.0 all-gather.3.cloned.1.call-done
  86.8 0.0 copy-start.1
  86.8 3.5 %fusion.19 = bf16[1,16,8,512]{3,2,0,1:T(8,128)(2,1)S(1)} fusion(bf16[128,2048]{0,1:T(8,128)(2,1)S(1)} %bitcast.61, bf16[1,2048,1024]{2,1,0:T(8,128)(2,1)} %all-gather.3.cloned.1.call-done, bf16[1,1024,512]{2,1,0:T(8,128)(2,1)} %param.13), kind=kOutput, calls=%fused_computation.15 | convolution fusion | flops 671416320 | bytes 5898240 | tf_op jit(solution)/shard_map/dot_general | solution.py:39
  90.2 20.2 %all_to_all.26 = bf16[1,16,8,512]{3,2,0,1:T(8,128)(2,1)S(1)} all-to-all(bf16[1,16,8,512]{3,2,0,1:T(8,128)(2,1)S(1)} %fusion.19), channel_id=1, replica_groups=mesh['tower'=16,'dev'=16] {'tower'}, dimensions={1} | all-to-all | bytes 262144 | tf_op jit(solution)/shard_map/all_to_all | solution.py:42
  110.5 0.1 copy.21
  110.6 0.2 convolution_multiply_fusion
  110.8 0.1 reshape.35
  110.9 0.0 copy-done
  110.9 0.4 fusion.29
  111.3 0.0 copy-done.1
  111.3 0.8 fusion.22
  (3 shorter events, 0.1 us)
Async XLA Ops:
  6.5 104.3 %copy-start = (bf16[8192,128]{1,0:T(8,128)(2,1)S(1)}, bf16[8192,128]{1,0:T(8,128)(2,1)}, u32[]{:S(2)}) copy-start(bf16[8192,128]{1,0:T(8,128)(2,1)} %param.14) | copy-start | bytes 6291460
  6.5 80.2 %all-gather.3.cloned.1.call-start = ((), (), s32[]{:S(2)}) async-start(), calls=%async_computation.2 | async-start | bytes 4456448 | tf_op jit(solution)/shard_map/all_gather | solution.py:35
  63.8 6.5 %copy-start.2 = (s32[2048]{0:T(1024)S(1)}, s32[2048]{0:T(1024)}, u32[]{:S(2)}) copy-start(s32[2048]{0:T(1024)} %param.11) | copy-start | bytes 24580
  86.8 24.5 %copy-start.1 = (f32[256,128]{1,0:T(8,128)S(1)}, f32[256,128]{1,0:T(8,128)}, u32[]{:S(2)}) copy-start(f32[256,128]{1,0:T(8,128)} %param.15) | copy-start | bytes 393220
Sparse Core Ops, SparseCore 0:
  9.2 43.9 all-gather.2
where the time goes:
time: 119 us
  other arithmetic  45.3 us (38%)
  blocking collectives  36.6 us (31%)
  between operations  13.5 us (11%)
  local copies, waits for them, and re-layouts  12.9 us (11%)
  matrix products  9.84 us (8%)
    reduce_sum x4, other arithmetic, pool_block(): jnp.sum((block_ids[:, :, None] == positions).astype(jnp.int32), axis=1)  44.5 us
    all_to_all x1, blocking collectives, on_device(): lax.all_to_all(outputs.reshape(1, towers, share, width), 'tower', split_a...  20.2 us
    all_to_all x1, blocking collectives, on_device(): lax.all_to_all(features, 'dev', split_axis=0, concat_axis=1, tiled=True)  16.4 us
    gather x2, local copies, waits for them, and re-layouts, on_device(): features = jnp.take(pieces, order, axis=0)  6.46 us
    dot_general x4, matrix products, pool_block(): jnp.dot(tally.astype(jnp.bfloat16), table, preferred_element_type=jnp.flo...  5.05 us
    eq x4, local copies, waits for them, and re-layouts, pool_block(): block_ids[:, :, None] == positions  3.88 us
    dot_general x1, matrix products, on_device(): jnp.dot(hidden, w_second[0], preferred_element_type=jnp.float32)  3.47 us
  transfers between devices with their start and end apart: 1, of which 0 were waited for; matrix products, arithmetic and copies ran while one was open for 53% of the time, Pallas kernels for 0%

commit v1 on v0

--- a/solution.py
+++ b/solution.py
@@ -39,8 +39,16 @@
     outputs = jnp.dot(hidden, w_second[0], preferred_element_type=jnp.float32).astype(jnp.bfloat16)
     width = outputs.shape[1]
     share = my_rows // towers
-    gathered = lax.all_to_all(
-        outputs.reshape(1, towers, share, width), "tower", split_axis=1, concat_axis=0, tiled=True
+    gathered = jnp.concatenate(
+        lax.all_to_all(
+            jnp.stack(
+                jnp.split(outputs.reshape(1, towers, share, width), lax.axis_size("tower"), axis=1)
+            ),
+            "tower",
+            0,
+            0,
+        ),
+        axis=0,
     )[:, 0]
     amount = gathered.shape[1]
     joined = jnp.transpose(gathered, (1, 0, 2)).reshape(amount, towers * width)

time: 119 us -> 119 us (level)
    unnamed x8 -> x23, local copies, waits for them, and re-layouts: 2.37 us -> 2.41 us
where the time goes in v1:
time: 119 us
  other arithmetic  45.3 us (38%)
  blocking collectives  36.6 us (31%)
  between operations  13.6 us (11%)
  local copies, waits for them, and re-layouts  12.9 us (11%)
  matrix products  9.84 us (8%)
    reduce_sum x4, other arithmetic, pool_block(): jnp.sum((block_ids[:, :, None] == positions).astype(jnp.int32), axis=1)  44.5 us
    all_to_all x1, blocking collectives, on_device(): lax.all_to_all(jnp.stack(jnp.split(outputs.reshape(1, towers, share, widt...  20.2 us
    all_to_all x1, blocking collectives, on_device(): lax.all_to_all(features, 'dev', split_axis=0, concat_axis=1, tiled=True)  16.4 us
    gather x2, local copies, waits for them, and re-layouts, on_device(): features = jnp.take(pieces, order, axis=0)  6.46 us
    dot_general x4, matrix products, pool_block(): jnp.dot(tally.astype(jnp.bfloat16), table, preferred_element_type=jnp.flo...  5.05 us
    eq x4, local copies, waits for them, and re-layouts, pool_block(): block_ids[:, :, None] == positions  3.88 us
    dot_general x1, matrix products, on_device(): jnp.dot(hidden, w_second[0], preferred_element_type=jnp.float32)  3.47 us
    unnamed x23, local copies, waits for them, and re-layouts  2.41 us
  transfers between devices with their start and end apart: 1, of which 0 were waited for; matrix products, arithmetic and copies ran while one was open for 53% of the time, Pallas kernels for 0%

profile of v1, /device:TPU:1, one launch (start us, length us, event | category | flops | bytes accessed | tf_op | source)
XLA Modules:
  0.0 119.1 jit_solution(6995948571340571670)
XLA Ops:
  6.5 0.0 copy-start
  6.5 0.0 all-gather.3.cloned.1.call-start
  6.5 0.7 all-gather.3.cloned.1.call-update
  7.3 2.3 %copy.300 = s32[1,1,2048,32]{3,2,1,0:T(8,128)} copy(s32[1,1,2048,32]{2,3,1,0:T(8,128)} %param.9) | data formatting | bytes 524288 | tf_op args[0]
  9.5 0.7 fusion.27
  10.2 53.5 %while.11 = (s32[]{:T(128)}, bf16[4,512,128]{2,1,0:T(8,128)(2,1)S(1)}, s32[4,512,32]{2,1,0:T(8,128)}, bf16[512,128]{1,0:T(8,128)(2,1)}, s32[]{:T(128)}) while((s32[]{:T(128)}, bf16[4,512,128]{2,1,0:T(8,128)(2,1)S(1)}, s32[4,512,32]{2,1,0:T(8,128)}, bf16[512,128]{1,0:T(8,128)(2,1)}, s32[]{:T(128)}) %tuple.27), condition=%wide.region_2.3_spmd.clone, body=%wide.region_0.2_spmd.clone.sunk | while | flops 92340224 | bytes 2555973 | solution.py:21
  10.2 1.0 dynamic-slice_bitcast_fusion.2
  11.2 11.1 %convert_reduce_fusion.2 = s32[512,512]{1,0:T(8,128)S(1)} fusion(s32[512,32]{1,0:T(8,128)S(1)} %dynamic-slice_bitcast_fusion.2), kind=kLoop, calls=%fused_computation.3.clone.1 | loop fusion | flops 24903680 | bytes 1114112 | tf_op jit(solution)/shard_map/while/body/eval_jaxpr/reduce_sum | solution.py:16
  22.4 1.3 %fusion.41 = bf16[4,512,128]{2,1,0:T(8,128)(2,1)S(1)} fusion(bf16[4,512,128]{2,1,0:T(8,128)(2,1)S(1)} %get-tuple-element.82, s32[]{:T(128)} %get-tuple-element.81, bf16[512,128]{1,0:T(8,128)(2,1)} %get-tuple-element.89, s32[512,512]{1,0:T(8,128)S(1)} %convert_reduce_fusion.2), kind=kOutput, calls=%fused_computation.6.clone.1 | convolution fusion | flops 67436544 | bytes 1310724 | tf_op jit(solution)/shard_map/while/body/eval_jaxpr/dot_general | solution.py:17
  23.6 1.0 dynamic-slice_bitcast_fusion.2
  24.6 11.1 %convert_reduce_fusion.2 = s32[512,512]{1,0:T(8,128)S(1)} fusion(s32[512,32]{1,0:T(8,128)S(1)} %dynamic-slice_bitcast_fusion.2), kind=kLoop, calls=%fused_computation.3.clone.1 | loop fusion | flops 24903680 | bytes 1114112 | tf_op jit(solution)/shard_map/while/body/eval_jaxpr/reduce_sum | solution.py:16
  35.7 1.3 %fusion.41 = bf16[4,512,128]{2,1,0:T(8,128)(2,1)S(1)} fusion(bf16[4,512,128]{2,1,0:T(8,128)(2,1)S(1)} %get-tuple-element.82, s32[]{:T(128)} %get-tuple-element.81, bf16[512,128]{1,0:T(8,128)(2,1)} %get-tuple-element.89, s32[512,512]{1,0:T(8,128)S(1)} %convert_reduce_fusion.2), kind=kOutput, calls=%fused_computation.6.clone.1 | convolution fusion | flops 67436544 | bytes 1310724 | tf_op jit(solution)/shard_map/while/body/eval_jaxpr/dot_general | solution.py:17
  37.0 1.0 dynamic-slice_bitcast_fusion.2
  38.0 11.1 %convert_reduce_fusion.2 = s32[512,512]{1,0:T(8,128)S(1)} fusion(s32[512,32]{1,0:T(8,128)S(1)} %dynamic-slice_bitcast_fusion.2), kind=kLoop, calls=%fused_computation.3.clone.1 | loop fusion | flops 24903680 | bytes 1114112 | tf_op jit(solution)/shard_map/while/body/eval_jaxpr/reduce_sum | solution.py:16
  49.1 1.3 %fusion.41 = bf16[4,512,128]{2,1,0:T(8,128)(2,1)S(1)} fusion(bf16[4,512,128]{2,1,0:T(8,128)(2,1)S(1)} %get-tuple-element.82, s32[]{:T(128)} %get-tuple-element.81, bf16[512,128]{1,0:T(8,128)(2,1)} %get-tuple-element.89, s32[512,512]{1,0:T(8,128)S(1)} %convert_reduce_fusion.2), kind=kOutput, calls=%fused_computation.6.clone.1 | convolution fusion | flops 67436544 | bytes 1310724 | tf_op jit(solution)/shard_map/while/body/eval_jaxpr/dot_general | solution.py:17
  50.4 1.0 dynamic-slice_bitcast_fusion.2
  51.4 11.1 %convert_reduce_fusion.2 = s32[512,512]{1,0:T(8,128)S(1)} fusion(s32[512,32]{1,0:T(8,128)S(1)} %dynamic-slice_bitcast_fusion.2), kind=kLoop, calls=%fused_computation.3.clone.1 | loop fusion | flops 24903680 | bytes 1114112 | tf_op jit(solution)/shard_map/while/body/eval_jaxpr/reduce_sum | solution.py:16
  62.5 1.3 %fusion.41 = bf16[4,512,128]{2,1,0:T(8,128)(2,1)S(1)} fusion(bf16[4,512,128]{2,1,0:T(8,128)(2,1)S(1)} %get-tuple-element.82, s32[]{:T(128)} %get-tuple-element.81, bf16[512,128]{1,0:T(8,128)(2,1)} %get-tuple-element.89, s32[512,512]{1,0:T(8,128)S(1)} %convert_reduce_fusion.2), kind=kOutput, calls=%fused_computation.6.clone.1 | convolution fusion | flops 67436544 | bytes 1310724 | tf_op jit(solution)/shard_map/while/body/eval_jaxpr/dot_general | solution.py:17
  63.8 0.0 copy-start.2
  63.8 6.2 %gather_fusion = bf16[2048,128]{1,0:T(8,128)(2,1)S(1)} fusion(bf16[2048,128]{1,0:T(8,128)(2,1)S(1)} %bitcast.120, s32[2048]{0:T(1024)S(1)} %fusion.27), kind=kCustom, calls=%fused_computation | custom fusion | bytes 1056768 | tf_op jit(solution)/shard_map/jit(_take)/gather | solution.py:31
  70.0 0.3 copy.301
  70.3 0.0 copy-done.2
  70.3 0.1 broadcast_select_fusion
  70.4 16.4 %all_to_all.21 = bf16[16,128,128]{1,2,0:T(8,128)(2,1)S(1)} all-to-all(bf16[16,128,128]{1,2,0:T(8,128)(2,1)S(1)} %broadcast_select_fusion), channel_id=1, replica_groups=mesh['tower'=16,'dev'=16] {'dev'}, dimensions={0} | all-to-all | bytes 1048576 | tf_op jit(solution)/shard_map/all_to_all | solution.py:32
  86.8 0.0 all-gather.3.cloned.1.call-done
  86.8 0.0 copy-start.1
  86.8 3.5 %fusion.19 = bf16[1,16,8,512]{3,2,1,0:T(8,128)(2,1)S(1)} fusion(bf16[128,2048]{0,1:T(8,128)(2,1)S(1)} %bitcast.123, bf16[1,2048,1024]{2,1,0:T(8,128)(2,1)} %all-gather.3.cloned.1.call-done, bf16[1,1024,512]{2,1,0:T(8,128)(2,1)} %param.13), kind=kOutput, calls=%fused_computation.15 | convolution fusion | flops 671416320 | bytes 5898240 | tf_op jit(solution)/shard_map/dot_general | solution.py:39
  90.4 20.2 %all_to_all.22 = bf16[16,1,1,8,512]{4,3,2,1,0:T(8,128)(2,1)S(1)} all-to-all(bf16[16,1,1,8,512]{4,3,2,1,0:T(8,128)(2,1)S(1)} %constant_dynamic-update-slice_fusion), channel_id=1, replica_groups=mesh['tower'=16,'dev'=16] {'tower'}, dimensions={0} | all-to-all | bytes 262144 | tf_op jit(solution)/shard_map/all_to_all | solution.py:43
  110.7 0.1 copy.303
  110.8 0.2 convolution_multiply_fusion
  111.0 0.1 reshape.31
  111.1 0.0 copy-done
  111.1 0.4 fusion.29
  111.5 0.0 copy-done.1
  111.5 0.8 fusion.22
  (19 shorter events, 0.1 us)
Async XLA Ops:
  6.5 104.5 %copy-start = (bf16[8192,128]{1,0:T(8,128)(2,1)S(1)}, bf16[8192,128]{1,0:T(8,128)(2,1)}, u32[]{:S(2)}) copy-start(bf16[8192,128]{1,0:T(8,128)(2,1)} %param.14) | copy-start | bytes 6291460
  6.5 80.2 %all-gather.3.cloned.1.call-start = ((), (), s32[]{:S(2)}) async-start(), calls=%async_computation.2 | async-start | bytes 4456448 | tf_op jit(solution)/shard_map/all_gather | solution.py:35
  63.8 6.5 %copy-start.2 = (s32[2048]{0:T(1024)S(1)}, s32[2048]{0:T(1024)}, u32[]{:S(2)}) copy-start(s32[2048]{0:T(1024)} %param.11) | copy-start | bytes 24580
  86.8 24.7 %copy-start.1 = (f32[256,128]{1,0:T(8,128)S(1)}, f32[256,128]{1,0:T(8,128)}, u32[]{:S(2)}) copy-start(f32[256,128]{1,0:T(8,128)} %param.15) | copy-start | bytes 393220
Sparse Core Ops, SparseCore 0:
  9.2 43.9 all-gather.2
